TPU v7x, 32 devices: a whole 2x2x4 slice. The times are simulated.
32 devices in a mesh: section: 2 (over y), dp: 4 (over x, core), mp: 4 (over z).
Axes of the slice: x: 2, y: 2, z: 4, core: 2. Of those that a mesh axis runs over, the one named last changes fastest.
Arguments:
- patches: bfloat16 [4096, 1280], P(('section', 'dp')), may hold values from -6 to 6
- patch_counts: int32 [16], P(('section', 'dp')), may hold values from 64 to 256, as said below
- dest_rows: int32 [1024], P(('section', 'dp')), may hold values from 0 to 4095, as said below
- qkv_weight: bfloat16 [1280, 3, 1280], P(None, None, 'mp'), may hold values from -1 to 1
- out_weight: bfloat16 [1280, 1280], P('mp'), may hold values from -0.15625 to 0.15625
- attn_gain: bfloat16 [1280], replicated, may hold values from 0.25 to 1.75
- merge_gain: bfloat16 [1280], replicated, may hold values from 0.25 to 1.75
- fc1_weight: bfloat16 [5120, 5120], P('mp', ('section', 'dp')), may hold values from -0.078125 to 0.078125
- fc1_bias: bfloat16 [5120], P(('section', 'dp')), may hold values from -3 to 3
- fc2_weight: bfloat16 [5120, 8192], P(('section', 'dp'), 'mp'), may hold values from -0.078125 to 0.078125
- fc2_bias: bfloat16 [8192], P('mp'), may hold values from -3 to 3
- text_embeds: bfloat16 [4096, 8192], P(('section', 'dp'), 'mp'), may hold values from -6 to 6
- section_hidden: bfloat16 [4096, 8192], P(('section', 'dp'), 'mp'), may hold values from -80 to 80
- llm_gain: bfloat16 [8192], P('mp'), may hold values from 0.25 to 1.75
Outputs:
- sequence_embeds: bfloat16 [4096, 8192], P(('section', 'dp'), 'mp')
- layer_inputs: bfloat16 [4096, 8192], P(('section', 'dp'), 'mp')
Inputs may be any that keep to these rules, and one draw needn't show every extreme that they name: `patch_counts`: multiples of 4; a tile's patches fill the first slots of its block. `dest_rows`: all rows differ. Each group's merged slots form runs of 16 consecutive slots (aligned); a run goes to one sequence slice (row // 512, numbered in section-major order), different runs of a group to different slices. Rows of slots that are not live are never written.
All inputs are finite; a program needn't handle non-finite values.
Results may differ from a plain program's by a relative error of at most 0.0055.
Values may be sent and summed in bfloat16 or wider, within the bound.
A program may use at most 128 MiB of HBM per device.

v0:
```python
import jax
import jax.numpy as jnp
from jax import lax
from jax.sharding import PartitionSpec as P

HEAD_DIM = 80
HID = 8192
vit_eps = 1e-06
llm_eps = 1e-06


def from_behind(value, axis, steps):
    count = lax.axis_size(axis)
    first, last = (max(0, -steps), min(count, count - steps))
    return lax.ppermute(value, axis, [(source, source + steps) for source in range(first, last)])


def layer_norm(values, gain):
    centred = values.astype(jnp.float32)
    centred = centred - jnp.mean(centred, axis=-1, keepdims=True)
    variance = jnp.mean(centred * centred, axis=-1, keepdims=True)
    return centred * lax.rsqrt(variance + vit_eps) * gain.astype(jnp.float32)


def per_device(
    patches,
    patch_counts,
    dest_rows,
    qkv_weight,
    out_weight,
    attn_gain,
    merge_gain,
    fc1_weight,
    fc1_bias,
    fc2_weight,
    fc2_bias,
    text_embeds,
    section_hidden,
    llm_gain,
):
    width = patches.shape[1]
    tile_total = patch_counts.shape[0]
    block_rows = patches.shape[0] // tile_total
    merged_rows = patches.shape[0] // 4
    local_cols = qkv_weight.shape[2]
    local_heads = local_cols // HEAD_DIM
    feature_cols = text_embeds.shape[1]
    seq_rows = text_embeds.shape[0]
    section_count = lax.axis_size("section")
    group_count = section_count * lax.axis_size("dp")
    run_cap = max(2, merged_rows // group_count)
    run_total = merged_rows // run_cap
    normed_in = layer_norm(patches, attn_gain).astype(jnp.bfloat16)
    projections = jnp.dot(
        normed_in, qkv_weight.reshape(width, 3 * local_cols), preferred_element_type=jnp.float32
    ).astype(jnp.bfloat16)
    projections = projections.reshape(tile_total, block_rows, 3, local_heads, HEAD_DIM)
    query_part = projections[:, :, 0]
    key_part = projections[:, :, 1]
    value_part = projections[:, :, 2]
    scores = jnp.einsum(
        "tqhd,tkhd->thqk", query_part, key_part, preferred_element_type=jnp.float32
    ) * HEAD_DIM ** (-0.5)
    key_live = (
        jnp.arange(block_rows, dtype=jnp.int32)[None, None, None, :]
        < patch_counts[:, None, None, None]
    )
    scores = jnp.where(key_live, scores, -1e30)
    weights = jax.nn.softmax(scores, axis=-1).astype(jnp.bfloat16)
    attended = jnp.einsum(
        "thqk,tkhd->tqhd", weights, value_part, preferred_element_type=jnp.float32
    ).astype(jnp.bfloat16)
    attended = attended.reshape(patches.shape[0], local_cols)
    partial_proj = jnp.dot(attended, out_weight, preferred_element_type=jnp.float32)
    position = lax.axis_index("mp")
    own_patch = lax.dynamic_slice_in_dim(
        patches.reshape(merged_rows, 4, width), position, 1, 1
    ).reshape(merged_rows, width)
    own_proj = lax.psum_scatter(
        partial_proj.reshape(merged_rows, 4, width), "mp", scatter_dimension=1, tiled=True
    ).reshape(merged_rows, width)
    block_out = (own_patch.astype(jnp.float32) + own_proj).astype(jnp.bfloat16)
    merge_part = layer_norm(block_out, merge_gain).astype(jnp.bfloat16)
    first_full, second_full, bias_full = (
        lax.all_gather(fc1_weight, "section", axis=1, tiled=True),
        lax.all_gather(fc2_weight, "section", axis=0, tiled=True),
        lax.all_gather(fc1_bias, "section", axis=0, tiled=True),
    )
    first_partial = jnp.dot(
        lax.all_gather(merge_part, "dp", axis=0, tiled=True),
        first_full,
        preferred_element_type=jnp.float32,
    )
    first_total = lax.psum(first_partial, "mp")
    hidden = jax.nn.gelu(first_total + bias_full.astype(jnp.float32), approximate=False).astype(
        jnp.bfloat16
    )
    embed_total = lax.psum_scatter(
        jnp.dot(hidden, second_full, preferred_element_type=jnp.float32).astype(jnp.bfloat16),
        "dp",
        scatter_dimension=0,
        tiled=True,
    ).astype(jnp.float32)
    image_embeds = (embed_total + fc2_bias.astype(jnp.float32)).astype(jnp.bfloat16)
    slot_in_tile = jnp.arange(merged_rows, dtype=jnp.int32) % (block_rows // 4)
    tile_counts = jnp.repeat(patch_counts, block_rows // 4, total_repeat_length=merged_rows)
    live = slot_in_tile * 4 < tile_counts
    receiver = dest_rows // seq_rows
    run_target = receiver.reshape(run_total, run_cap)[:, 0]
    place = jnp.where(live, dest_rows % seq_rows, seq_rows)
    send_rows = (
        jnp.zeros((group_count, run_cap, feature_cols), jnp.bfloat16)
        .at[run_target]
        .set(image_embeds.reshape(run_total, run_cap, feature_cols))
    )
    send_place = (
        jnp.full((group_count, run_cap), seq_rows, jnp.int32)
        .at[run_target]
        .set(place.reshape(run_total, run_cap))
    )
    got_rows, got_place = (
        lax.all_to_all(send_rows, ("section", "dp"), split_axis=0, concat_axis=0, tiled=True),
        lax.all_to_all(send_place, ("section", "dp"), split_axis=0, concat_axis=0, tiled=True),
    )
    sequence_embeds = text_embeds.at[got_place.reshape(-1)].set(
        got_rows.reshape(-1, feature_cols), mode="drop"
    )
    incoming = from_behind(section_hidden, "section", 1)
    entering = jnp.where(lax.axis_index("section") == 0, sequence_embeds, incoming).astype(
        jnp.float32
    )
    row_total = lax.psum(jnp.sum(entering * entering, axis=1), "mp")
    layer_inputs = (
        entering * lax.rsqrt(row_total / HID + llm_eps)[:, None] * llm_gain.astype(jnp.float32)
    ).astype(jnp.bfloat16)
    return (sequence_embeds, layer_inputs)


def solution(mesh):
    in_specs = (
        P(("section", "dp"), None),
        P(("section", "dp")),
        P(("section", "dp")),
        P(None, None, "mp"),
        P("mp", None),
        P(),
        P(),
        P("mp", ("section", "dp")),
        P(("section", "dp")),
        P(("section", "dp"), "mp"),
        P("mp"),
        P(("section", "dp"), "mp"),
        P(("section", "dp"), "mp"),
        P("mp"),
    )
    out_specs = (P(("section", "dp"), "mp"), P(("section", "dp"), "mp"))
    return jax.shard_map(
        per_device, mesh=mesh, in_specs=in_specs, out_specs=out_specs, check_vma=False
    )
```

profile of v0, /device:TPU:0, one launch (start us, length us, event | category | flops | bytes accessed | tf_op | source)
XLA Modules:
  0.0 317.5 jit_solution(10290408837068384715)
XLA Ops:
  8.0 0.0 copy-start
  8.0 0.0 reduce-scatter.3.cloned.1.call-start
  8.1 0.0 copy-start.1
  8.1 3.3 %copy.70 = bf16[512,2048]{1,0:T(8,128)(2,1)} copy(bf16[512,2048]{1,0:T(8,128)(2,1)} %param.27) | data formatting | bytes 4194304
  11.4 0.2 convert_reduce_fusion
  11.7 0.5 fusion.6
  12.2 2.6 convolution_convert_fusion.1
  14.8 2.5 reshape.162
  17.3 1.6 fusion.107
  18.9 0.1 iota_compare_fusion
  18.9 3.3 %fusion.109 = (f32[2,4,256]{2,1,0:T(4,128)S(1)}, f32[2,4,256,256]{2,3,1,0:T(8,128)}) fusion(pred[2,256]{1,0:T(4,128)(4,1)S(1)} %iota_compare_fusion, bf16[2,256,1,4,80]{1,0,4,3,2:T(2,128)(2,1)} %get-tuple-element.18, bf16[2,256,1,4,80]{1,0,4,3,2:T(2,128)(2,1)} %get-tuple-element.17), kind=kOutput, calls=%fused_computation.154 | convolution fusion | flops 85983488 | bytes 2761216 | tf_op jit(solution)/shard_map/sub | solution.py:69
  22.2 1.9 fusion.56
  24.1 0.3 copy.33
  24.4 0.5 dot_general.23
  24.9 3.5 %fusion.60 = f32[128,4,1280]{2,0,1:T(8,128)} fusion(bf16[320,1280]{1,0:T(8,128)(2,1)} %param.20, bf16[128,4,320]{2,1,0:T(4,128)(2,1)S(1)} %dot_general.23), kind=kOutput, calls=%fused_computation.82 | convolution fusion | flops 419430400 | bytes 3768320 | tf_op jit(solution)/shard_map/dot_general | solution.py:74
  28.4 0.0 reduce-scatter.3.cloned.1.call-update
  28.5 0.0 copy-start.4
  28.5 0.0 all-gather.7.cloned.1.call-start
  28.5 0.5 all-gather.7.cloned.1.call-update
  29.1 0.0 all-gather.5.cloned.1.call-start
  29.1 3.5 %reshape.160 = bf16[128,4,1280]{2,1,0:T(4,128)(2,1)} reshape(bf16[512,1280]{1,0:T(8,128)(2,1)} %param.16) | data formatting | bytes 2621440 | tf_op jit(solution)/shard_map/reshape | solution.py:77
  32.6 2.0 constant_dynamic-slice_fusion
  34.6 49.0 %reduce-scatter.3.cloned.1.call-done = f32[128,1,1280]{2,0,1:T(8,128)} async-done(((f32[128,4,1280]{2,0,1:T(8,128)}), f32[128,1,1280]{2,0,1:T(8,128)}) %reduce-scatter.3.cloned.1.call-update) | async-done | bytes 655376 | tf_op jit(solution)/shard_map/reduce_scatter | solution.py:79
  83.6 1.2 convert_reduce_fusion.1
  84.8 0.2 fusion.65
  85.1 1.0 fusion.67
  86.0 0.0 all-gather.5.cloned.1.call-update
  86.1 0.0 all-gather.9.cloned.1.call-start
  86.1 0.5 all-gather.9.cloned.1.call-update
  86.6 0.0 all-reduce.2.cloned.1.call-start
  86.7 0.0 all-gather.7.cloned.1.call-done
  86.7 17.1 %all-gather.5.cloned.1.call-done = bf16[512,1280]{1,0:T(8,128)(2,1)} async-done(((bf16[128,1280]{1,0:T(8,128)(2,1)}), bf16[512,1280]{1,0:T(8,128)(2,1)}) %all-gather.5.cloned.1.call-update) | async-done | bytes 1310736 | tf_op jit(solution)/shard_map/all_gather | solution.py:90
  103.8 5.8 %fusion.110 = f32[512,1280]{1,0:T(8,128)} fusion(bf16[512,1280]{1,0:T(8,128)(2,1)} %all-gather.5.cloned.1.call-done, bf16[1280,1280]{1,0:T(8,128)(2,1)} %all-gather.7.cloned.1.call-done), kind=kOutput, calls=%fused_computation.155 | convolution fusion | flops 1677721600 | bytes 7208960 | tf_op jit(solution)/shard_map/dot_general | solution.py:89
  109.6 0.0 all-reduce.2.cloned.1.call-update
  109.6 0.0 reduce-scatter.5.cloned.1.call-start
  109.6 0.6 copy-done.7
  110.2 4.5 %all-gather = bf16[2,1,640]{2,1,0:T(2,128)(2,1)S(1)} all-gather(bf16[1,1,640]{2,1,0:T(2,128)(2,1)S(1)} %reshape.198), channel_id=1, replica_groups=mesh['section'=2,'dp'=4,'mp'=4] {'section'}, dimensions={0}, use_global_device_ids=true | all-gather | bytes 3840 | tf_op jit(solution)/shard_map/all_gather | solution.py:87
  114.8 0.0 copy-start.10
  114.8 58.8 %all-gather.9.cloned.1.call-done = bf16[1280,2048]{1,0:T(8,128)(2,1)} async-done(((bf16[640,2048]{1,0:T(8,128)(2,1)}), bf16[1280,2048]{1,0:T(8,128)(2,1)}) %all-gather.9.cloned.1.call-update) | async-done | bytes 5242896 | tf_op jit(solution)/shard_map/all_gather | solution.py:86
  173.6 40.2 %all-reduce.2.cloned.1.call-done = f32[512,1280]{1,0:T(8,128)} async-done(((f32[512,1280]{1,0:T(8,128)}), f32[512,1280]{1,0:T(8,128)}) %all-reduce.2.cloned.1.call-update) | async-done | bytes 2621456 | tf_op jit(solution)/shard_map/psum | solution.py:94
  213.8 12.1 %convolution_convert_fusion = bf16[512,2048]{1,0:T(8,128)(2,1)} fusion(bf16[1280,2048]{1,0:T(8,128)(2,1)} %all-gather.9.cloned.1.call-done, f32[512,1280]{1,0:T(8,128)} %all-reduce.2.cloned.1.call-done, f32[1280]{0:T(1024)S(1)} %reshape.200), kind=kOutput, calls=%fused_computation.14 | convolution fusion | flops 2728656896 | bytes 9966592 | tf_op jit(solution)/shard_map/dot_general | solution.py:99
  225.9 0.0 reduce-scatter.5.cloned.1.call-update
  225.9 4.7 %collective-permute-start = (bf16[512,2048]{1,0:T(8,128)(2,1)}, bf16[512,2048]{1,0:T(8,128)(2,1)}, u32[]{:S(2)}, u32[]{:S(2)}) collective-permute-start(bf16[512,2048]{1,0:T(8,128)(2,1)} %param.28), channel_id=1, source_target_pairs={{0,16},{1,17},{2,18},{3,19},{4,20},{5,21},{6,22},{7,23},{8,24},{9,... | collective-permute-start | bytes 6291464 | tf_op jit(solution)/shard_map/ppermute | solution.py:15
  230.7 0.6 fusion.108
  231.3 1.3 compare_select_fusion.2
  232.6 0.1 reshape.157
  232.6 0.1 reshape.178
  232.7 0.1 fusion.70
  232.8 1.2 scatter_custom_fusion
  234.0 3.3 %all-to-all-start = ((s32[8,1,16]{2,1,0:T(1,128)}), s32[8,1,16]{2,1,0:T(1,128)S(1)}, u32[]{:S(2)}, u32[]{:S(2)}) async-start(s32[8,1,16]{2,1,0:T(1,128)} %bitcast.3), calls=%async_computation | async-start | bytes 8192 | tf_op jit(solution)/shard_map/all_to_all | solution.py:123
  237.3 19.0 %reduce-scatter.5.cloned.1.call-done = bf16[128,2048]{1,0:T(8,128)(2,1)} async-done(((bf16[512,2048]{1,0:T(8,128)(2,1)}), bf16[128,2048]{1,0:T(8,128)(2,1)}) %reduce-scatter.5.cloned.1.call-update) | async-done | bytes 524304 | tf_op jit(solution)/shard_map/reduce_scatter | solution.py:98
  256.3 1.1 add_convert_fusion
  257.4 0.8 broadcast_in_dim.20
  258.3 2.4 scatter_fusion
  260.7 13.7 %all-to-all-done = s32[8,1,16]{2,1,0:T(1,128)S(1)} async-done(((s32[8,1,16]{2,1,0:T(1,128)}), s32[8,1,16]{2,1,0:T(1,128)S(1)}, u32[]{:S(2)}, u32[]{:S(2)}) %all-to-all-start) | async-done | bytes 544 | tf_op jit(solution)/shard_map/all_to_all | solution.py:123
  274.4 4.7 %all-to-all-start.1 = ((bf16[8,16,2048]{2,1,0:T(8,128)(2,1)}), bf16[8,16,2048]{2,1,0:T(8,128)(2,1)S(1)}, u32[]{:S(2)}, u32[]{:S(2)}) async-start(bf16[8,16,2048]{2,1,0:T(8,128)(2,1)} %scatter_fusion), calls=%async_computation.3 | async-start | bytes 1048576 | tf_op jit(solution)/shard_map/all_to_all | solution.py:122
  279.1 0.5 broadcast.190
  279.6 0.6 reduce.10
  280.2 0.1 reshape.159
  280.3 8.5 %all-to-all-done.1 = bf16[8,16,2048]{2,1,0:T(8,128)(2,1)S(1)} async-done(((bf16[8,16,2048]{2,1,0:T(8,128)(2,1)}), bf16[8,16,2048]{2,1,0:T(8,128)(2,1)S(1)}, u32[]{:S(2)}, u32[]{:S(2)}) %all-to-all-start.1) | async-done | bytes 524320 | tf_op jit(solution)/shard_map/all_to_all | solution.py:122
  288.8 4.6 %scatter_fusion.1 = bf16[512,2048]{1,0:T(8,128)(2,1)} fusion(bf16[512,2048]{1,0:T(8,128)(2,1)} %copy.70, s32[128]{0:T(128)S(1)} %fusion.74, bf16[128,2048]{1,0:T(8,128)(2,1)S(1)} %bitcast.61), kind=kCustom, calls=%fused_computation.2 | custom fusion | bytes 1573376 | tf_op jit(solution)/shard_map/scatter | solution.py:125
  293.4 2.3 fusion.1
  295.7 10.0 %psum.15 = f32[512]{0:T(512)S(1)} all-reduce(f32[512]{0:T(512)S(1)} %fusion.1), channel_id=1, replica_groups=mesh['section'=2,'dp'=4,'mp'=4] {'mp'}, use_global_device_ids=true, to_apply=%region_13.14 | all-reduce | flops 512 | bytes 4096 | tf_op jit(solution)/shard_map/psum | solution.py:132
  305.8 4.1 %fusion.3 = bf16[512,2048]{1,0:T(8,128)(2,1)} fusion(f32[2048]{0:T(1024)S(1)} %convert_element_type.88, f32[512]{0:T(512)S(1)} %add_rsqrt_fusion, bf16[512,2048]{1,0:T(8,128)(2,1)} %scatter_fusion.1, bf16[512,2048]{1,0:T(8,128)(2,1)} %collective-permute-done, pred[]{:T(512)S(6)} %eq.6), kind=kLoop, calls=%fused_computation.8 | loop fusion | flops 5242880 | bytes 6301697 | tf_op jit(solution)/shard_map/convert_element_type | solution.py:135
  (31 shorter events, 0.1 us)
Async XLA Ops:
  8.0 4.2 %copy-start = (bf16[1280,3,320]{0,2,1:T(8,128)(2,1)S(1)}, bf16[1280,3,320]{0,2,1:T(8,128)(2,1)}, u32[]{:S(2)}) copy-start(bf16[1280,3,320]{0,2,1:T(8,128)(2,1)} %param.19) | copy-start | bytes 7372804
  8.0 4.1 %copy-start.3 = (bf16[1280]{0:T(1024)(128)(2,1)S(1)}, bf16[1280]{0:T(1024)(128)(2,1)}, u32[]{:S(2)}) copy-start(bf16[1280]{0:T(1024)(128)(2,1)} %param.21) | copy-start | bytes 7684
  8.0 75.6 %reduce-scatter.3.cloned.1.call-start = ((), (), s32[]{:S(2)}) async-start(), calls=%async_computation.4 | async-start | bytes 3276800 | tf_op jit(solution)/shard_map/reduce_scatter | solution.py:79
  8.1 3.3 %copy-start.1 = (bf16[512,1280]{1,0:T(8,128)(2,1)S(1)}, bf16[512,1280]{1,0:T(8,128)(2,1)}, u32[]{:S(2)}) copy-start(bf16[512,1280]{1,0:T(8,128)(2,1)} %param.16) | copy-start | bytes 3932164
  14.8 4.1 %copy-start.8 = (s32[2]{0:T(128)S(1)}, s32[2]{0:T(128)}, u32[]{:S(2)}) copy-start(s32[2]{0:T(128)} %param.17) | copy-start | bytes 28
  18.9 3.4 %copy-start.2 = (bf16[2,256,1,4,80]{1,0,4,3,2:T(2,128)(2,1)S(1)}, bf16[2,256,1,4,80]{1,0,4,3,2:T(2,128)(2,1)}, u32[]{:S(2)}) copy-start(bf16[2,256,1,4,80]{1,0,4,3,2:T(2,128)(2,1)} %get-tuple-element.16) | copy-start | bytes 983044
  28.5 4.1 %copy-start.4 = (bf16[1280]{0:T(1024)(128)(2,1)S(1)}, bf16[1280]{0:T(1024)(128)(2,1)}, u32[]{:S(2)}) copy-start(bf16[1280]{0:T(1024)(128)(2,1)} %param.22) | copy-start | bytes 7684
  28.5 58.3 %all-gather.7.cloned.1.call-start = ((), (), s32[]{:S(2)}) async-start(), calls=%async_computation.6 | async-start | bytes 4915200 | tf_op jit(solution)/shard_map/all_gather | solution.py:85
  29.1 74.7 %all-gather.5.cloned.1.call-start = ((), (), s32[]{:S(2)}) async-start(), calls=%async_computation.5 | async-start | bytes 1638400 | tf_op jit(solution)/shard_map/all_gather | solution.py:90
  86.1 87.6 %all-gather.9.cloned.1.call-start = ((), (), s32[]{:S(2)}) async-start(), calls=%async_computation.8 | async-start | bytes 7864320 | tf_op jit(solution)/shard_map/all_gather | solution.py:86
  86.6 127.2 %all-reduce.2.cloned.1.call-start = ((), (), s32[]{:S(2)}) async-start(), calls=%async_computation.7 | async-start | bytes 5242880 | tf_op jit(solution)/shard_map/psum | solution.py:94
  109.5 0.7 copy-start.7
  109.6 146.7 %reduce-scatter.5.cloned.1.call-start = ((), (), s32[]{:S(2)}) async-start(), calls=%async_computation.9 | async-start | bytes 2621440 | tf_op jit(solution)/shard_map/reduce_scatter | solution.py:98
  114.8 116.5 %copy-start.9 = (s32[128]{0:T(128)S(1)}, s32[128]{0:T(128)}, u32[]{:S(2)}) copy-start(s32[128]{0:T(128)} %param.18) | copy-start | bytes 1540
  114.8 116.5 %copy-start.10 = (pred[128]{0:T(512)(128)(4,1)S(1)}, pred[128]{0:T(512)(128)(4,1)}, u32[]{:S(2)}) copy-start(pred[128]{0:T(512)(128)(4,1)} %constant.224) | copy-start | bytes 388
  114.8 122.4 %copy-start.5 = (bf16[2048]{0:T(1024)(128)(2,1)S(1)}, bf16[2048]{0:T(1024)(128)(2,1)}, u32[]{:S(2)}) copy-start(bf16[2048]{0:T(1024)(128)(2,1)} %param.26) | copy-start | bytes 12292
  225.9 53.1 %copy-start.6 = (bf16[2048]{0:T(1024)(128)(2,1)S(1)}, bf16[2048]{0:T(1024)(128)(2,1)}, u32[]{:S(2)}) copy-start(bf16[2048]{0:T(1024)(128)(2,1)} %param.29) | copy-start | bytes 12292
  225.9 67.4 %collective-permute-start = (bf16[512,2048]{1,0:T(8,128)(2,1)}, bf16[512,2048]{1,0:T(8,128)(2,1)}, u32[]{:S(2)}, u32[]{:S(2)}) collective-permute-start(bf16[512,2048]{1,0:T(8,128)(2,1)} %param.28), channel_id=1, source_target_pairs={{0,16},{1,17},{2,18},{3,19},{4,20},{5,21},{6,22},{7,23},{8,24},{9,... | collective-permute-start | bytes 6291464 | tf_op jit(solution)/shard_map/ppermute | solution.py:15
  234.0 40.4 %all-to-all-start = ((s32[8,1,16]{2,1,0:T(1,128)}), s32[8,1,16]{2,1,0:T(1,128)S(1)}, u32[]{:S(2)}, u32[]{:S(2)}) async-start(s32[8,1,16]{2,1,0:T(1,128)} %bitcast.3), calls=%async_computation | async-start | bytes 8192 | tf_op jit(solution)/shard_map/all_to_all | solution.py:123
  274.4 14.4 %all-to-all-start.1 = ((bf16[8,16,2048]{2,1,0:T(8,128)(2,1)}), bf16[8,16,2048]{2,1,0:T(8,128)(2,1)S(1)}, u32[]{:S(2)}, u32[]{:S(2)}) async-start(bf16[8,16,2048]{2,1,0:T(8,128)(2,1)} %scatter_fusion), calls=%async_computation.3 | async-start | bytes 1048576 | tf_op jit(solution)/shard_map/all_to_all | solution.py:122
Sparse Core Ops, SparseCore 0:
  28.6 54.9 reduce-scatter.2
  109.7 104.0 all-reduce.1
Sparse Core Ops, SparseCore 1:
  30.5 48.9 all-gather.6
  86.2 17.6 all-gather.4
  105.2 68.4 all-gather.8
  226.0 30.2 reduce-scatter.4
where the time goes:
time: 318 us; the launch traced here: 317 us
  waiting for transfers between devices  207 us (65%)
  matrix products  29.1 us (9%)
  local copies, waits for them, and re-layouts  24.8 us (8%)
  between operations  15.9 us (5%)
  blocking collectives  14.6 us (5%)
  starting transfers between devices  12.9 us (4%)
  other arithmetic  12.9 us (4%)
    all_gather x1, waiting for transfers between devices, per_device(): lax.all_gather(fc2_weight, 'section', axis=0, tiled=True)  58.8 us
    reduce_scatter x1, waiting for transfers between devices, per_device(): lax.psum_scatter(partial_proj.reshape(merged_rows, 4, width), 'mp', scatt...  49 us
    psum x1, waiting for transfers between devices, per_device(): first_total = lax.psum(first_partial, 'mp')  40.2 us
    reduce_scatter x1, waiting for transfers between devices, per_device(): lax.psum_scatter(jnp.dot(hidden, second_full, preferred_element_type=jnp....  19 us
    all_gather x1, waiting for transfers between devices, per_device(): lax.all_gather(merge_part, 'dp', axis=0, tiled=True)  17.1 us
    all_to_all x1, waiting for transfers between devices, per_device(): lax.all_to_all(send_place, ('section', 'dp'), split_axis=0, concat_axis=0...  13.7 us
    dot_general x1, matrix products, per_device(): jnp.dot(hidden, second_full, preferred_element_type=jnp.float32)  12.1 us
    psum x1, blocking collectives, per_device(): row_total = lax.psum(jnp.sum(entering * entering, axis=1), 'mp')  10 us
  transfers between devices with their start and end apart: 9, of which 7 were waited for; matrix products, arithmetic and copies ran while one was open for 9% of the time, Pallas kernels for 0%

commit v1 on v0

--- a/solution.py
+++ b/solution.py
@@ -91,7 +91,7 @@
         first_full,
         preferred_element_type=jnp.float32,
     )
-    first_total = lax.psum(first_partial, "mp")
+    first_total = jnp.sum(lax.all_gather(first_partial, "mp"), axis=0)
     hidden = jax.nn.gelu(first_total + bias_full.astype(jnp.float32), approximate=False).astype(
         jnp.bfloat16
     )

time: 318 us -> 467 us (1.47)
  waiting for transfers between devices: 207 us -> 350 us
  other arithmetic: 12.9 us -> 19.4 us
    all_gather x0 -> x1, waiting for transfers between devices: none -> 179 us  [per_device(): first_total = jnp.sum(lax.all_gather(first_partial, 'mp'), axis=0)]
    psum x1 -> x0, waiting for transfers between devices: 40.2 us -> none  [per_device(): first_total = lax.psum(first_partial, 'mp')]
    reduce_sum x0 -> x1, other arithmetic: none -> 6.43 us  [per_device(): first_total = jnp.sum(lax.all_gather(first_partial, 'mp'), axis=0)]
  transfers between devices with their start and end apart: 9 -> 9, of which waited for: 7 -> 7; matrix products, arithmetic and copies ran while one was open for 9% -> 6% of each run, Pallas kernels for 0% -> 0%
where the time goes in v1:
time: 467 us; the launch traced here: 466 us
  waiting for transfers between devices  350 us (75%)
  matrix products  29.1 us (6%)
  local copies, waits for them, and re-layouts  24.2 us (5%)
  other arithmetic  19.4 us (4%)
  blocking collectives  16.2 us (3%)
  between operations  15.6 us (3%)
  starting transfers between devices  11.8 us (3%)
    all_gather x1, waiting for transfers between devices, per_device(): first_total = jnp.sum(lax.all_gather(first_partial, 'mp'), axis=0)  179 us
    all_gather x1, waiting for transfers between devices, per_device(): lax.all_gather(fc2_weight, 'section', axis=0, tiled=True)  61.9 us
    reduce_scatter x1, waiting for transfers between devices, per_device(): lax.psum_scatter(partial_proj.reshape(merged_rows, 4, width), 'mp', scatt...  49 us
    reduce_scatter x1, waiting for transfers between devices, per_device(): lax.psum_scatter(jnp.dot(hidden, second_full, preferred_element_type=jnp....  21.1 us
    all_gather x1, waiting for transfers between devices, per_device(): lax.all_gather(merge_part, 'dp', axis=0, tiled=True)  17.6 us
    dot_general x1, matrix products, per_device(): jnp.dot(hidden, second_full, preferred_element_type=jnp.float32)  12.1 us
    all_to_all x1, waiting for transfers between devices, per_device(): lax.all_to_all(send_place, ('section', 'dp'), split_axis=0, concat_axis=0...  11.8 us
    psum x1, blocking collectives, per_device(): row_total = lax.psum(jnp.sum(entering * entering, axis=1), 'mp')  11.7 us
  transfers between devices with their start and end apart: 9, of which 7 were waited for; matrix products, arithmetic and copies ran while one was open for 6% of the time, Pallas kernels for 0%

profile of v1, /device:TPU:0, one launch (start us, length us, event | category | flops | bytes accessed | tf_op | source)
XLA Modules:
  0.0 466.0 jit_solution(1850547975907895341)
XLA Ops:
  8.0 0.0 copy-start
  8.0 0.0 reduce-scatter.3.cloned.1.call-start
  8.1 0.0 copy-start.1
  8.1 3.3 copy.69
  11.4 0.2 convert_reduce_fusion
  11.7 0.5 fusion.6
  12.2 2.6 convolution_convert_fusion.1
  14.8 2.5 reshape.162
  17.3 1.6 fusion.107
  18.9 0.1 iota_compare_fusion
  18.9 3.3 fusion.109
  22.2 1.9 fusion.56
  24.1 0.3 copy.33
  24.4 0.5 dot_general.23
  24.9 3.5 fusion.60
  28.5 0.0 reduce-scatter.3.cloned.1.call-update
  28.5 0.0 copy-start.4
  28.5 0.0 all-gather.9.cloned.1.call-start
  28.6 0.5 all-gather.9.cloned.1.call-update
  29.1 0.0 all-gather.7.cloned.1.call-start
  29.1 3.5 reshape.160
  32.6 2.0 constant_dynamic-slice_fusion
  34.6 49.0 %reduce-scatter.3.cloned.1.call-done = f32[128,1,1280]{2,0,1:T(8,128)} async-done(((f32[128,4,1280]{2,0,1:T(8,128)}), f32[128,1,1280]{2,0,1:T(8,128)}) %reduce-scatter.3.cloned.1.call-update) | async-done | bytes 655376 | tf_op jit(solution)/shard_map/reduce_scatter | solution.py:79
  83.6 1.2 convert_reduce_fusion.1
  84.9 0.2 fusion.65
  85.1 1.0 fusion.67
  86.1 0.0 all-gather.7.cloned.1.call-update
  86.1 0.0 all-gather.13.cloned.1.call-start
  86.1 0.0 all-gather.9.cloned.1.call-done
  86.2 17.6 %all-gather.7.cloned.1.call-done = bf16[512,1280]{1,0:T(8,128)(2,1)} async-done(((bf16[128,1280]{1,0:T(8,128)(2,1)}), bf16[512,1280]{1,0:T(8,128)(2,1)}) %all-gather.7.cloned.1.call-update) | async-done | bytes 1310736 | tf_op jit(solution)/shard_map/all_gather | solution.py:90
  103.8 5.7 %fusion.110 = f32[512,1280]{1,0:T(8,128)} fusion(bf16[512,1280]{1,0:T(8,128)(2,1)} %all-gather.7.cloned.1.call-done, bf16[1280,1280]{1,0:T(8,128)(2,1)} %all-gather.9.cloned.1.call-done), kind=kOutput, calls=%fused_computation.155 | convolution fusion | flops 1677721600 | bytes 7208960 | tf_op jit(solution)/shard_map/dot_general | solution.py:89
  109.5 0.0 all-gather.13.cloned.1.call-update
  109.5 0.0 all-gather.11.cloned.1.call-start
  109.6 0.7 all-gather.11.cloned.1.call-update
  110.2 0.0 reduce-scatter.5.cloned.1.call-start
  110.3 4.5 all-gather.1
  114.9 178.7 %all-gather.13.cloned.1.call-done = f32[2048,1280]{1,0:T(8,128)} async-done(((f32[512,1280]{1,0:T(8,128)}), f32[2048,1280]{1,0:T(8,128)}) %all-gather.13.cloned.1.call-update) | async-done | bytes 10485776 | tf_op jit(solution)/shard_map/all_gather | solution.py:94
  293.6 6.4 %reduce_sum.68 = f32[512,1280]{1,0:T(8,128)} reduce(f32[4,512,1280]{2,1,0:T(8,128)} %bitcast.62, f32[]{:T(128)} %constant.182.clone.1), dimensions={0}, to_apply=%region_8.9 | reduce | flops 1966080 | bytes 13107204 | tf_op jit(solution)/shard_map/reduce_sum | solution.py:94
  300.0 61.9 %all-gather.11.cloned.1.call-done = bf16[1280,2048]{1,0:T(8,128)(2,1)} async-done(((bf16[640,2048]{1,0:T(8,128)(2,1)}), bf16[1280,2048]{1,0:T(8,128)(2,1)}) %all-gather.11.cloned.1.call-update) | async-done | bytes 5242896 | tf_op jit(solution)/shard_map/all_gather | solution.py:86
  361.9 12.1 %convolution_convert_fusion = bf16[512,2048]{1,0:T(8,128)(2,1)} fusion(bf16[1280,2048]{1,0:T(8,128)(2,1)} %all-gather.11.cloned.1.call-done, f32[512,1280]{1,0:T(8,128)} %reduce_sum.68, f32[1280]{0:T(1024)S(1)} %reshape.201), kind=kOutput, calls=%fused_computation.14 | convolution fusion | flops 2728656896 | bytes 9966592 | tf_op jit(solution)/shard_map/dot_general | solution.py:99
  374.0 0.0 reduce-scatter.5.cloned.1.call-update
  374.0 0.0 copy-start.6
  374.0 3.6 collective-permute-start
  377.6 0.6 fusion.108
  378.2 1.3 compare_select_fusion.2
  379.5 0.1 reshape.157
  379.6 0.1 reshape.178
  379.6 0.1 fusion.70
  379.8 1.2 scatter_custom_fusion
  380.9 3.3 all-to-all-start
  384.2 21.1 %reduce-scatter.5.cloned.1.call-done = bf16[128,2048]{1,0:T(8,128)(2,1)} async-done(((bf16[512,2048]{1,0:T(8,128)(2,1)}), bf16[128,2048]{1,0:T(8,128)(2,1)}) %reduce-scatter.5.cloned.1.call-update) | async-done | bytes 524304 | tf_op jit(solution)/shard_map/reduce_scatter | solution.py:98
  405.3 1.1 add_convert_fusion
  406.5 0.8 broadcast_in_dim.20
  407.3 2.4 scatter_fusion
  409.7 11.8 %all-to-all-done = s32[8,1,16]{2,1,0:T(1,128)S(1)} async-done(((s32[8,1,16]{2,1,0:T(1,128)}), s32[8,1,16]{2,1,0:T(1,128)S(1)}, u32[]{:S(2)}, u32[]{:S(2)}) %all-to-all-start) | async-done | bytes 544 | tf_op jit(solution)/shard_map/all_to_all | solution.py:123
  421.5 4.7 %all-to-all-start.1 = ((bf16[8,16,2048]{2,1,0:T(8,128)(2,1)}), bf16[8,16,2048]{2,1,0:T(8,128)(2,1)S(1)}, u32[]{:S(2)}, u32[]{:S(2)}) async-start(bf16[8,16,2048]{2,1,0:T(8,128)(2,1)} %scatter_fusion), calls=%async_computation.3 | async-start | bytes 1048576 | tf_op jit(solution)/shard_map/all_to_all | solution.py:122
  426.2 0.5 broadcast.190
  426.7 0.6 reduce.10
  427.4 0.1 reshape.159
  427.5 8.5 %all-to-all-done.1 = bf16[8,16,2048]{2,1,0:T(8,128)(2,1)S(1)} async-done(((bf16[8,16,2048]{2,1,0:T(8,128)(2,1)}), bf16[8,16,2048]{2,1,0:T(8,128)(2,1)S(1)}, u32[]{:S(2)}, u32[]{:S(2)}) %all-to-all-start.1) | async-done | bytes 524320 | tf_op jit(solution)/shard_map/all_to_all | solution.py:122
  435.9 4.6 scatter_fusion.1
  440.5 2.3 fusion.1
  442.9 11.7 %psum.7 = f32[512]{0:T(512)S(1)} all-reduce(f32[512]{0:T(512)S(1)} %fusion.1), channel_id=1, replica_groups=mesh['section'=2,'dp'=4,'mp'=4] {'mp'}, use_global_device_ids=true, to_apply=%region_13.14 | all-reduce | flops 512 | bytes 4096 | tf_op jit(solution)/shard_map/psum | solution.py:132
  454.6 4.1 fusion.3
  (32 shorter events, 0.1 us)
Async XLA Ops:
  8.0 4.2 copy-start
  8.0 4.1 copy-start.3
  8.0 75.6 %reduce-scatter.3.cloned.1.call-start = ((), (), s32[]{:S(2)}) async-start(), calls=%async_computation.4 | async-start | bytes 3276800 | tf_op jit(solution)/shard_map/reduce_scatter | solution.py:79
  8.1 3.3 copy-start.1
  14.8 4.1 copy-start.8
  18.9 3.4 copy-start.2
  28.5 4.1 copy-start.4
  28.5 57.7 %all-gather.9.cloned.1.call-start = ((), (), s32[]{:S(2)}) async-start(), calls=%async_computation.6 | async-start | bytes 4915200 | tf_op jit(solution)/shard_map/all_gather | solution.py:85
  29.1 74.7 %all-gather.7.cloned.1.call-start = ((), (), s32[]{:S(2)}) async-start(), calls=%async_computation.5 | async-start | bytes 1638400 | tf_op jit(solution)/shard_map/all_gather | solution.py:90
  86.1 207.5 %all-gather.13.cloned.1.call-start = ((), (), s32[]{:S(2)}) async-start(), calls=%async_computation.9 | async-start | bytes 13107200 | tf_op jit(solution)/shard_map/all_gather | solution.py:94
  109.5 0.8 copy-start.7
  109.5 252.4 %all-gather.11.cloned.1.call-start = ((), (), s32[]{:S(2)}) async-start(), calls=%async_computation.7 | async-start | bytes 7864320 | tf_op jit(solution)/shard_map/all_gather | solution.py:86
  110.2 295.1 %reduce-scatter.5.cloned.1.call-start = ((), (), s32[]{:S(2)}) async-start(), calls=%async_computation.8 | async-start | bytes 2621440 | tf_op jit(solution)/shard_map/reduce_scatter | solution.py:98
  300.0 78.2 %copy-start.9 = (s32[128]{0:T(128)S(1)}, s32[128]{0:T(128)}, u32[]{:S(2)}) copy-start(s32[128]{0:T(128)} %param.18) | copy-start | bytes 1540
  300.0 78.2 %copy-start.10 = (pred[128]{0:T(512)(128)(4,1)S(1)}, pred[128]{0:T(512)(128)(4,1)}, u32[]{:S(2)}) copy-start(pred[128]{0:T(512)(128)(4,1)} %constant.224) | copy-start | bytes 388
  300.0 84.2 %copy-start.5 = (bf16[2048]{0:T(1024)(128)(2,1)S(1)}, bf16[2048]{0:T(1024)(128)(2,1)}, u32[]{:S(2)}) copy-start(bf16[2048]{0:T(1024)(128)(2,1)} %param.26) | copy-start | bytes 12292
  374.0 52.2 %copy-start.6 = (bf16[2048]{0:T(1024)(128)(2,1)S(1)}, bf16[2048]{0:T(1024)(128)(2,1)}, u32[]{:S(2)}) copy-start(bf16[2048]{0:T(1024)(128)(2,1)} %param.29) | copy-start | bytes 12292
  374.0 66.5 %collective-permute-start = (bf16[512,2048]{1,0:T(8,128)(2,1)}, bf16[512,2048]{1,0:T(8,128)(2,1)}, u32[]{:S(2)}, u32[]{:S(2)}) collective-permute-start(bf16[512,2048]{1,0:T(8,128)(2,1)} %param.28), channel_id=1, source_target_pairs={{0,16},{1,17},{2,18},{3,19},{4,20},{5,21},{6,22},{7,23},{8,24},{9,... | collective-permute-start | bytes 6291464 | tf_op jit(solution)/shard_map/ppermute | solution.py:15
  380.9 40.6 %all-to-all-start = ((s32[8,1,16]{2,1,0:T(1,128)}), s32[8,1,16]{2,1,0:T(1,128)S(1)}, u32[]{:S(2)}, u32[]{:S(2)}) async-start(s32[8,1,16]{2,1,0:T(1,128)} %bitcast.3), calls=%async_computation | async-start | bytes 8192 | tf_op jit(solution)/shard_map/all_to_all | solution.py:123
  421.5 14.4 %all-to-all-start.1 = ((bf16[8,16,2048]{2,1,0:T(8,128)(2,1)}), bf16[8,16,2048]{2,1,0:T(8,128)(2,1)S(1)}, u32[]{:S(2)}, u32[]{:S(2)}) async-start(bf16[8,16,2048]{2,1,0:T(8,128)(2,1)} %scatter_fusion), calls=%async_computation.3 | async-start | bytes 1048576 | tf_op jit(solution)/shard_map/all_to_all | solution.py:122
Sparse Core Ops, SparseCore 0:
  28.6 54.9 reduce-scatter.2
  109.6 183.8 all-gather.12
  295.1 66.7 all-gather.10
Sparse Core Ops, SparseCore 1:
  30.5 48.9 all-gather.8
  86.2 17.6 all-gather.6
  374.1 31.2 reduce-scatter.4
